TPU v7x, 128 devices: a whole 4x4x4 slice. The times are simulated.
128 devices in a mesh: seq: 8 (over y, core), span: 16 (over x, z).
Axes of the slice: x: 4, y: 4, z: 4, core: 2. Of those that a mesh axis runs over, the one named last changes fastest.
Arguments:
- queries: bfloat16 [16, 1024, 1536], P('span', 'seq'), may hold values from -6 to 6
- key_head_matrix: bfloat16 [16, 1024, 512], P('span', 'seq'), may hold values from -6 to 6
- value_head_matrix: bfloat16 [16, 1024, 512], P('span', 'seq'), may hold values from -6 to 6
- attn_output: bfloat16 [16, 1024, 1536], P('span', 'seq'), may hold values from -6 to 6
- out_grad: bfloat16 [16, 1024, 1536], P('span', 'seq'), may hold values from -6 to 6
Outputs:
- query_grad: bfloat16 [16, 1024, 1536], P('span', 'seq')
- key_grad: bfloat16 [16, 1024, 512], P('span', 'seq')
- value_grad: bfloat16 [16, 1024, 512], P('span', 'seq')
All inputs are finite; a program needn't handle non-finite values.
Results may differ from a plain program's by a relative error of at most 0.005.
Values may be sent and summed in bfloat16 or wider, within the bound.
A program may use at most 64 MiB of HBM per device.

v0:
```python
import math
import jax
import jax.numpy as jnp
from jax import lax
from jax.sharding import PartitionSpec as P

HEAD_WIDTH = 64
QUERY_PER_KEY = 3
NEG_LARGE = -1e30


def sent_together(arrays, axis, dim, along):
    ends, at = ([], 0)
    for a in arrays[:-1]:
        at += a.shape[along]
        ends.append(at)
    both = jnp.concatenate(arrays, axis=along)
    return tuple(
        jnp.split(lax.psum_scatter(both, axis, scatter_dimension=dim, tiled=True), ends, axis=along)
    )


def spread_rows(source, seq_count):
    return source.reshape(source.shape[1], seq_count, source.shape[2] // seq_count)


def over_blocks(update, running, arrays, offset, block_rows, live_test):
    row_total = arrays[0].shape[0]
    block_total = row_total // block_rows

    def visit(block_number, running_state):
        first_row = block_number * block_rows
        slices = tuple(
            (lax.dynamic_slice_in_dim(member, first_row, block_rows, 0) for member in arrays)
        )
        position = offset + first_row
        return lax.cond(
            live_test(position),
            lambda current: update(current, slices, position),
            lambda current: current,
            running_state,
        )

    return lax.fori_loop(0, block_total, visit, running)


def per_device(queries, key_head_matrix, value_head_matrix, attn_output, out_grad):
    seq_count = lax.axis_size("seq")
    own_block = lax.axis_index("span")
    tok_local = queries.shape[1]
    kv_local = key_head_matrix.shape[2] // (HEAD_WIDTH * seq_count)
    block_len = tok_local * seq_count
    scaling = 1.0 / math.sqrt(HEAD_WIDTH)
    exchanged = (
        lax.all_to_all(
            spread_rows(queries, seq_count), "seq", split_axis=1, concat_axis=0, tiled=True
        ),
        lax.all_to_all(
            spread_rows(out_grad, seq_count), "seq", split_axis=1, concat_axis=0, tiled=True
        ),
        lax.all_to_all(
            spread_rows(attn_output, seq_count), "seq", split_axis=1, concat_axis=0, tiled=True
        ),
        lax.all_to_all(
            spread_rows(key_head_matrix, seq_count), "seq", split_axis=1, concat_axis=0, tiled=True
        ),
        lax.all_to_all(
            spread_rows(value_head_matrix, seq_count),
            "seq",
            split_axis=1,
            concat_axis=0,
            tiled=True,
        ),
    )
    query_flat = exchanged[0].reshape(block_len, kv_local * QUERY_PER_KEY * HEAD_WIDTH)
    grad_flat = exchanged[1].reshape(block_len, kv_local * QUERY_PER_KEY * HEAD_WIDTH)
    query_split = query_flat.reshape(block_len, kv_local, QUERY_PER_KEY, HEAD_WIDTH)
    grad_split = grad_flat.reshape(block_len, kv_local, QUERY_PER_KEY, HEAD_WIDTH)
    output_split = exchanged[2].reshape(block_len, kv_local, QUERY_PER_KEY, HEAD_WIDTH)
    key_flat = exchanged[3].reshape(block_len, kv_local * HEAD_WIDTH)
    value_flat = exchanged[4].reshape(block_len, kv_local * HEAD_WIDTH)
    row_delta = jnp.transpose(
        jnp.sum(grad_split.astype(jnp.float32) * output_split.astype(jnp.float32), axis=3),
        (1, 2, 0),
    )
    own_first = own_block * block_len
    query_pos = own_first + lax.iota(jnp.int32, block_len)

    def key_live(position):
        return position < own_first + block_len

    def key_scores(key_block, position):
        rows_here = key_block.shape[0]
        key_split = key_block.reshape(rows_here, kv_local, HEAD_WIDTH)
        scores = (
            jnp.einsum("tgjd,rgd->gjtr", query_split, key_split, preferred_element_type=jnp.float32)
            * scaling
        )
        key_pos = position + lax.iota(jnp.int32, rows_here)
        allowed = key_pos[None, :] <= query_pos[:, None]
        return (key_split, scores, allowed)

    def stats_update(running_state, slices, position):
        row_max, row_sum = running_state
        key_split, scores, allowed = key_scores(slices[0], position)
        masked = jnp.where(allowed, scores, NEG_LARGE)
        new_max = jnp.maximum(row_max, jnp.max(masked, axis=3))
        weights = jnp.where(allowed, jnp.exp(scores - new_max[..., None]), 0.0)
        new_sum = row_sum * jnp.exp(row_max - new_max) + jnp.sum(weights, axis=3)
        return (new_max, new_sum)

    stats_init = (
        jnp.full((kv_local, QUERY_PER_KEY, block_len), NEG_LARGE, jnp.float32),
        jnp.zeros((kv_local, QUERY_PER_KEY, block_len), jnp.float32),
    )
    key_whole, value_whole = (
        lax.all_gather(key_flat, "span", axis=0, tiled=True),
        lax.all_gather(value_flat, "span", axis=0, tiled=True),
    )
    row_max, row_sum = over_blocks(stats_update, stats_init, (key_whole,), 0, block_len, key_live)
    log_norm = row_max + jnp.log(row_sum)

    def key_side(slices, position):
        key_split, scores, allowed = key_scores(slices[0], position)
        value_split = slices[1].reshape(slices[1].shape[0], kv_local, HEAD_WIDTH)
        prob_weights = jnp.where(allowed, jnp.exp(scores - log_norm[..., None]), 0.0)
        prob_grad = jnp.einsum(
            "tgjd,rgd->gjtr", grad_split, value_split, preferred_element_type=jnp.float32
        )
        score_low = (prob_weights * (prob_grad - row_delta[..., None])).astype(jnp.bfloat16)
        query_term = scaling * jnp.einsum(
            "gjtr,rgd->tgjd", score_low, key_split, preferred_element_type=jnp.float32
        )
        return (prob_weights, score_low, query_term)

    def partial_update(running_state, slices, position):
        query_acc, key_acc, value_acc = running_state
        prob_weights, score_low, query_term = key_side(slices, position)
        rows_here = slices[0].shape[0]
        key_term = scaling * jnp.einsum(
            "gjtr,tgjd->rgd", score_low, query_split, preferred_element_type=jnp.float32
        )
        value_term = jnp.einsum(
            "gjtr,tgjd->rgd",
            prob_weights.astype(jnp.bfloat16),
            grad_split,
            preferred_element_type=jnp.float32,
        )
        key_acc = lax.dynamic_update_slice_in_dim(
            key_acc, key_term.reshape(rows_here, kv_local * HEAD_WIDTH), position, 0
        )
        value_acc = lax.dynamic_update_slice_in_dim(
            value_acc, value_term.reshape(rows_here, kv_local * HEAD_WIDTH), position, 0
        )
        return (query_acc + query_term, key_acc, value_acc)

    query_zero = jnp.zeros((block_len, kv_local, QUERY_PER_KEY, HEAD_WIDTH), jnp.float32)
    buffer_zero = jnp.zeros((lax.axis_size("span") * block_len, kv_local * HEAD_WIDTH), jnp.float32)
    grad_init = (query_zero, buffer_zero, buffer_zero)
    grad_result = over_blocks(
        partial_update, grad_init, (key_whole, value_whole), 0, block_len, key_live
    )
    query_acc, key_acc, value_acc = grad_result
    key_total, value_total = sent_together((key_acc, value_acc), "span", 0, 1)
    query_out = query_acc.astype(jnp.bfloat16).reshape(
        seq_count, tok_local, kv_local * QUERY_PER_KEY * HEAD_WIDTH
    )
    key_result = key_total.astype(jnp.bfloat16).reshape(seq_count, tok_local, kv_local * HEAD_WIDTH)
    value_result = value_total.astype(jnp.bfloat16).reshape(
        seq_count, tok_local, kv_local * HEAD_WIDTH
    )
    returned = (
        lax.all_to_all(query_out, "seq", split_axis=0, concat_axis=2, tiled=True),
        lax.all_to_all(key_result, "seq", split_axis=0, concat_axis=2, tiled=True),
        lax.all_to_all(value_result, "seq", split_axis=0, concat_axis=2, tiled=True),
    )
    return (returned[0], returned[1], returned[2])


def solution(mesh):
    in_specs = (
        P("span", "seq", None),
        P("span", "seq", None),
        P("span", "seq", None),
        P("span", "seq", None),
        P("span", "seq", None),
    )
    out_specs = (P("span", "seq", None), P("span", "seq", None), P("span", "seq", None))
    return jax.shard_map(
        per_device, mesh=mesh, in_specs=in_specs, out_specs=out_specs, check_vma=False
    )
```

profile of v0, /device:TPU:1, one launch (start us, length us, event | category | flops | bytes accessed | tf_op | source)
XLA Modules:
  0.0 670.2 jit_solution(363014363874218583)
XLA Ops:
  7.2 1.0 copy.53
  8.2 11.0 %all_to_all.123 = bf16[128,8,64]{0,2,1:T(8,128)(2,1)S(1)} all-to-all(bf16[128,8,64]{0,2,1:T(8,128)(2,1)S(1)} %bitcast.200), channel_id=1, replica_groups=mesh['seq'=8,'span'=16] {'seq'}, dimensions={1} | all-to-all | bytes 262144 | tf_op jit(solution)/shard_map/all_to_all | solution.py:64
  19.3 0.7 copy.86
  20.1 1.0 copy.57
  21.1 8.5 %all_to_all.124 = bf16[128,8,64]{0,2,1:T(8,128)(2,1)S(1)} all-to-all(bf16[128,8,64]{0,2,1:T(8,128)(2,1)S(1)} %bitcast.201), channel_id=1, replica_groups=mesh['seq'=8,'span'=16] {'seq'}, dimensions={1} | all-to-all | bytes 262144 | tf_op jit(solution)/shard_map/all_to_all | solution.py:67
  29.7 0.7 copy.85
  30.4 1.9 copy.55
  32.3 4.2 all-to-all-start.1
  36.5 1.9 copy.61
  38.5 5.8 all-to-all-done.1
  44.3 4.6 all-to-all-start.4
  48.8 1.9 copy.59
  50.7 5.9 all-to-all-done.4
  56.6 4.5 all-to-all-start.3
  61.6 0.5 copy.62
  62.1 6.8 %all-to-all-done.3 = bf16[128,8,192]{0,2,1:T(8,128)(2,1)S(1)} async-done(((bf16[128,8,192]{0,2,1:T(8,128)(2,1)}), bf16[128,8,192]{0,2,1:T(8,128)(2,1)S(1)}, u32[]{:S(2)}, u32[]{:S(2)}) %all-to-all-start.3) | async-done | bytes 393248 | tf_op jit(solution)/shard_map/all_to_all | solution.py:58
  70.0 9.1 %while.38 = (s32[]{:T(128)}, f32[1,3,1024]{2,1,0:T(4,128)S(1)}, f32[1,3,1024]{2,1,0:T(4,128)S(1)}, s32[]{:T(128)}, bf16[16384,64]{0,1:T(8,128)(2,1)}, /*index=5*...) while((s32[]{:T(128)}, f32[1,3,1024]{2,1,0:T(4,128)S(1)}, ...), condition=%wide.region_5.6_spmd.clone, body=%wide.region_0.5_spmd.clone.sunk | while | flops 425730048 | bytes 33214752 | solution.py:44
  70.0 8.2 %conditional.6 = ((f32[1,3,1024]{2,1,0:T(4,128)S(1)}, f32[1,3,1024]{2,1,0:T(4,128)S(1)})) conditional(s32[]{:T(128)} %convert_element_type.97, (f32[1,3,1024]{2,1,0:T(4,128)S(1)}, f32[1,3,1024]{2,1,0:T(4,128)S(1)}) %tuple.120, (s32[]{:T(128)}, s32[]{:T(128)}, bf16[16384,64]{0,1:T(8,128)(2,1)}, bf16[1024,1,3,64]{0,3,2,1:T(8,128)(2,1)S(1)}, ...), branch_computations={%region_1.1_spmd, %region_2.4_spmd} | conditional | flops 425730048 | bytes 33210466 | solution.py:37
  70.1 0.7 broadcast_compare_fusion
  70.7 3.6 fusion.4
  74.4 3.9 fusion.7
  79.1 32.2 %all-gather.5.cloned.1.call-done = bf16[16384,64]{0,1:T(8,128)(2,1)} async-done(((bf16[1024,64]{0,1:T(8,128)(2,1)}), bf16[16384,64]{0,1:T(8,128)(2,1)}) %all-gather.5.cloned.1.call-update) | async-done | bytes 2097168 | tf_op jit(solution)/shard_map/all_gather | solution.py:118
  111.3 1.0 broadcast_in_dim.49
  112.3 2.3 broadcast_in_dim.50.clone
  114.6 2.3 broadcast_in_dim.50
  116.9 21.9 %while.39 = (s32[]{:T(128)}, f32[1024,1,3,64]{0,3,2,1:T(8,128)}, f32[16384,64]{0,1:T(8,128)}, f32[16384,64]{0,1:T(8,128)}, s32[]{:T(128)}, /*index=5*/bf16[16384...) while((s32[]{:T(128)}, f32[1024,1,3,64]{0,3,2,1:T(8,128)}, ...), condition=%wide.region_10.11_spmd.clone, body=%wide.region_7.10_spmd.clone.sunk | while | flops 2046232576 | bytes 63893872 | solution.py:44
  116.9 21.1 %conditional.7 = ((f32[1024,1,3,64]{0,3,2,1:T(8,128)}, f32[16384,64]{0,1:T(8,128)}, f32[16384,64]{0,1:T(8,128)})) conditional(s32[]{:T(128)} %convert_element_type.98, (f32[1024,1,3,64]{0,3,2,1:T(8,128)}, f32[16384,64]{0,1:T(8,128)}, f32[16384,64]{0,1:T(8,128)}) %tuple.123, (s32[]{:T(128)}, bf16[16384,64]{0,1:T(8,128)(2,1)}, s32[]{:T(128)}, ...), branch_computations={%region_8.8_spmd, %region_9.9_spmd} | conditional | flops 2046232576 | bytes 63889500 | solution.py:37
  116.9 1.6 broadcast_compare_fusion.1
  118.5 2.7 fusion.36
  121.2 5.9 fusion.19
  127.1 4.9 fusion.30
  132.0 3.3 fusion.24
  135.3 2.7 fusion.26
  138.8 7.5 %pad_maximum_fusion = f32[16384,128]{0,1:T(8,128)} fusion(f32[16384,64]{0,1:T(8,128)} %get-tuple-element.679, f32[16384,64]{0,1:T(8,128)} %get-tuple-element.678), kind=kLoop, calls=%fused_computation.56 | loop fusion | flops 2097152 | bytes 16777216 | tf_op jit(solution)/shard_map/concatenate | solution.py:17
  146.3 1.2 convert_element_type.77
  147.6 0.8 copy.64
  148.4 6.5 all-to-all-start.5
  154.9 485.2 %reduce-scatter.2.cloned.1.call-done = f32[1024,128]{0,1:T(8,128)} async-done(((f32[16384,128]{0,1:T(8,128)}), f32[1024,128]{0,1:T(8,128)}) %reduce-scatter.2.cloned.1.call-update) | async-done | bytes 524304 | tf_op jit(solution)/shard_map/reduce_scatter | solution.py:19
  640.1 1.1 convert.7
  641.2 0.7 copy.87
  641.9 6.4 all-to-all-start.7
  648.3 0.7 copy.88
  648.9 4.6 all-to-all-done.7
  653.5 4.1 all-to-all-start.6
  657.6 0.9 copy.67
  658.6 0.8 copy.69
  659.3 3.6 all-to-all-done.6
  662.9 0.8 copy.68
  (92 shorter events, 2.6 us)
Async XLA Ops:
  7.2 62.4 %all-gather.3.cloned.1.call-start = ((), (), s32[]{:S(2)}) async-start(), calls=%async_computation.9 | async-start | bytes 2228224 | tf_op jit(solution)/shard_map/all_gather | solution.py:117
  20.0 91.3 %all-gather.5.cloned.1.call-start = ((), (), s32[]{:S(2)}) async-start(), calls=%async_computation.10 | async-start | bytes 2228224 | tf_op jit(solution)/shard_map/all_gather | solution.py:118
  32.3 11.9 %all-to-all-start.1 = ((bf16[128,8,192]{0,2,1:T(8,128)(2,1)}), bf16[128,8,192]{0,2,1:T(8,128)(2,1)S(1)}, u32[]{:S(2)}, u32[]{:S(2)}) async-start(bf16[128,8,192]{0,2,1:T(8,128)(2,1)} %bitcast.27), calls=%async_computation.1 | async-start | bytes 786432 | tf_op jit(solution)/shard_map/all_to_all | solution.py:55
  44.3 12.4 %all-to-all-start.4 = ((bf16[128,8,192]{0,2,1:T(8,128)(2,1)}), bf16[128,8,192]{0,2,1:T(8,128)(2,1)S(1)}, u32[]{:S(2)}, u32[]{:S(2)}) async-start(bf16[128,8,192]{0,2,1:T(8,128)(2,1)} %bitcast.36), calls=%async_computation.4 | async-start | bytes 786432 | tf_op jit(solution)/shard_map/all_to_all | solution.py:61
  56.6 12.2 %all-to-all-start.3 = ((bf16[128,8,192]{0,2,1:T(8,128)(2,1)}), bf16[128,8,192]{0,2,1:T(8,128)(2,1)S(1)}, u32[]{:S(2)}, u32[]{:S(2)}) async-start(bf16[128,8,192]{0,2,1:T(8,128)(2,1)} %bitcast.33), calls=%async_computation.3 | async-start | bytes 786432 | tf_op jit(solution)/shard_map/all_to_all | solution.py:58
  61.1 579.0 %reduce-scatter.2.cloned.1.call-start = ((), (), s32[]{:S(2)}) async-start(), calls=%async_computation.11 | async-start | bytes 8912896 | tf_op jit(solution)/shard_map/reduce_scatter | solution.py:19
  69.3 0.7 copy-start.1
  70.7 3.6 copy-start
  148.4 493.5 %all-to-all-start.5 = ((bf16[8,128,192]{1,2,0:T(8,128)(2,1)}), bf16[8,128,192]{1,2,0:T(8,128)(2,1)S(1)}, u32[]{:S(2)}, u32[]{:S(2)}) async-start(bf16[8,128,192]{1,2,0:T(8,128)(2,1)} %copy.64), calls=%async_computation.5 | async-start | bytes 786432 | tf_op jit(solution)/shard_map/all_to_all | solution.py:173
  641.9 11.6 %all-to-all-start.7 = ((bf16[8,128,64]{1,2,0:T(8,128)(2,1)}), bf16[8,128,64]{1,2,0:T(8,128)(2,1)S(1)}, u32[]{:S(2)}, u32[]{:S(2)}) async-start(bf16[8,128,64]{1,2,0:T(8,128)(2,1)} %bitcast.183), calls=%async_computation.8 | async-start | bytes 262144 | tf_op jit(solution)/shard_map/all_to_all | solution.py:175
  653.5 9.4 %all-to-all-start.6 = ((bf16[8,128,64]{1,2,0:T(8,128)(2,1)}), bf16[8,128,64]{1,2,0:T(8,128)(2,1)S(1)}, u32[]{:S(2)}, u32[]{:S(2)}) async-start(bf16[8,128,64]{1,2,0:T(8,128)(2,1)} %bitcast.184), calls=%async_computation.7 | async-start | bytes 262144 | tf_op jit(solution)/shard_map/all_to_all | solution.py:174
Sparse Core Ops, SparseCore 0:
  20.2 44.0 all-gather.2
  67.0 44.2 all-gather.4
  146.5 493.5 reduce-scatter.1
where the time goes:
time: 674 us; the launch traced here: 670 us
  waiting for transfers between devices  544 us (81%)
  starting transfers between devices  30.4 us (5%)
  matrix products  23.1 us (3%)
  local copies, waits for them, and re-layouts  21.5 us (3%)
  blocking collectives  19.5 us (3%)
  other arithmetic  16.3 us (2%)
  between operations  13.9 us (2%)
    reduce_scatter x1, waiting for transfers between devices, sent_together(): lax.psum_scatter(both, axis, scatter_dimension=dim, tiled=True)  485 us
    all_gather x1, waiting for transfers between devices, per_device(): lax.all_gather(value_flat, 'span', axis=0, tiled=True)  32.2 us
  transfers between devices with their start and end apart: 9, of which 7 were waited for; matrix products, arithmetic and copies ran while one was open for 4% of the time, Pallas kernels for 0%

commit v1 on v0

--- a/solution.py
+++ b/solution.py
@@ -115,7 +115,9 @@
     )
     key_whole, value_whole = (
         lax.all_gather(key_flat, "span", axis=0, tiled=True),
-        lax.all_gather(value_flat, "span", axis=0, tiled=True),
+        jnp.concatenate(
+            lax.all_to_all(jnp.stack([value_flat] * lax.axis_size("span")), "span", 0, 0), axis=0
+        ),
     )
     row_max, row_sum = over_blocks(stats_update, stats_init, (key_whole,), 0, block_len, key_live)
     log_norm = row_max + jnp.log(row_sum)

time: 674 us -> 709 us (1.052)
  waiting for transfers between devices: 544 us -> 566 us
  starting transfers between devices: 30.4 us -> 44.1 us
  blocking collectives: 19.5 us -> 11 us
    all_gather x1 -> x0, waiting for transfers between devices: 32.2 us -> none  [per_device(): lax.all_gather(value_flat, 'span', axis=0, tiled=True)]
    reduce_scatter x1, waiting for transfers between devices: 485 us -> 515 us  [sent_together(): lax.psum_scatter(both, axis, scatter_dimension=dim, tiled=True)]
    all_to_all x0 -> x2, waiting for transfers between devices: none -> 23 us  [the longest x1 19.6 us: per_device(): lax.all_to_all(jnp.stack([value_flat] * lax.axis_size('span')), 'span', 0...]
    all_to_all x0 -> x2, starting transfers between devices: none -> 11.7 us  [the longest x1 7.6 us: per_device(): lax.all_to_all(jnp.stack([value_flat] * lax.axis_size('span')), 'span', 0...]
    all_to_all x1 -> x0, blocking collectives: 8.49 us -> none  [per_device(): lax.all_to_all(spread_rows(value_head_matrix, seq_count), 'seq', split_ax...]
  transfers between devices with their start and end apart: 9 -> 10, of which waited for: 7 -> 8; matrix products, arithmetic and copies ran while one was open for 4% -> 3% of each run, Pallas kernels for 0% -> 0%
where the time goes in v1:
time: 709 us; the launch traced here: 705 us
  waiting for transfers between devices  566 us (80%)
  starting transfers between devices  44.1 us (6%)
  local copies, waits for them, and re-layouts  27.6 us (4%)
  matrix products  23.2 us (3%)
  other arithmetic  17.3 us (2%)
  between operations  14.2 us (2%)
  blocking collectives  11 us (2%)
    reduce_scatter x1, waiting for transfers between devices, sent_together(): lax.psum_scatter(both, axis, scatter_dimension=dim, tiled=True)  515 us
    all_to_all x1, waiting for transfers between devices, per_device(): lax.all_to_all(jnp.stack([value_flat] * lax.axis_size('span')), 'span', 0...  19.6 us
  transfers between devices with their start and end apart: 10, of which 8 were waited for; matrix products, arithmetic and copies ran while one was open for 3% of the time, Pallas kernels for 0%

profile of v1, /device:TPU:1, one launch (start us, length us, event | category | flops | bytes accessed | tf_op | source)
XLA Modules:
  0.0 704.6 jit_solution(8619097985235125774)
XLA Ops:
  7.2 1.0 copy.73
  8.2 11.0 %all_to_all.128 = bf16[128,8,64]{0,2,1:T(8,128)(2,1)S(1)} all-to-all(bf16[128,8,64]{0,2,1:T(8,128)(2,1)S(1)} %bitcast.204), channel_id=1, replica_groups=mesh['seq'=8,'span'=16] {'seq'}, dimensions={1} | all-to-all | bytes 262144 | tf_op jit(solution)/shard_map/all_to_all | solution.py:64
  20.0 1.7 copy.77
  21.7 4.1 all-to-all-start.2
  25.8 1.9 copy.75
  27.8 3.4 all-to-all-done.2
  31.1 4.2 all-to-all-start.1
  35.3 1.9 copy.82
  37.2 5.9 all-to-all-done.1
  43.1 4.5 all-to-all-start.5
  47.6 1.9 copy.80
  49.5 5.9 all-to-all-done.5
  55.4 4.5 all-to-all-start.4
  60.0 7.6 %all-to-all-done.4 = bf16[128,8,192]{0,2,1:T(8,128)(2,1)S(1)} async-done(((bf16[128,8,192]{0,2,1:T(8,128)(2,1)}), bf16[128,8,192]{0,2,1:T(8,128)(2,1)S(1)}, u32[]{:S(2)}, u32[]{:S(2)}) %all-to-all-start.4) | async-done | bytes 393248 | tf_op jit(solution)/shard_map/all_to_all | solution.py:58
  67.6 1.6 stack.3
  69.2 7.6 %all-to-all-start.3 = ((bf16[16,1024,64]{1,2,0:T(8,128)(2,1)}), bf16[16,1024,64]{1,2,0:T(8,128)(2,1)S(1)}, u32[]{:S(2)}, u32[]{:S(2)}) async-start(bf16[16,1024,64]{1,2,0:T(8,128)(2,1)} %stack.3), calls=%async_computation.3 | async-start | bytes 4194304 | tf_op jit(solution)/shard_map/all_to_all | solution.py:119
  77.9 2.0 copy.81
  79.9 1.9 reshape_reshape.7
  81.8 1.2 fusion.49
  83.0 19.6 %all-to-all-done.3 = bf16[16,1024,64]{1,2,0:T(8,128)(2,1)S(1)} async-done(((bf16[16,1024,64]{1,2,0:T(8,128)(2,1)}), bf16[16,1024,64]{1,2,0:T(8,128)(2,1)S(1)}, u32[]{:S(2)}, u32[]{:S(2)}) %all-to-all-start.3) | async-done | bytes 2097184 | tf_op jit(solution)/shard_map/all_to_all | solution.py:119
  102.6 1.5 copy.96
  104.2 9.1 %while.38 = (s32[]{:T(128)}, f32[1,3,1024]{2,1,0:T(4,128)S(1)}, f32[1,3,1024]{2,1,0:T(4,128)S(1)}, s32[]{:T(128)}, bf16[16384,64]{0,1:T(8,128)(2,1)}, /*index=5*...) while((s32[]{:T(128)}, f32[1,3,1024]{2,1,0:T(4,128)S(1)}, ...), condition=%wide.region_5.6_spmd.clone, body=%wide.region_0.5_spmd.clone.sunk | while | flops 425730048 | bytes 33214752 | solution.py:44
  104.2 8.3 %conditional.6 = ((f32[1,3,1024]{2,1,0:T(4,128)S(1)}, f32[1,3,1024]{2,1,0:T(4,128)S(1)})) conditional(s32[]{:T(128)} %convert_element_type.97, (f32[1,3,1024]{2,1,0:T(4,128)S(1)}, f32[1,3,1024]{2,1,0:T(4,128)S(1)}) %tuple.121, (s32[]{:T(128)}, s32[]{:T(128)}, bf16[16384,64]{0,1:T(8,128)(2,1)}, bf16[1024,1,3,64]{0,3,2,1:T(8,128)(2,1)S(1)}, ...), branch_computations={%region_1.1_spmd, %region_2.4_spmd} | conditional | flops 425730048 | bytes 33210466 | solution.py:37
  104.9 3.6 fusion.4
  108.5 3.9 fusion.7
  113.3 1.0 broadcast_in_dim.49
  114.3 2.3 broadcast_in_dim.50.clone
  116.6 2.3 broadcast_in_dim.50
  118.9 22.0 %while.39 = (s32[]{:T(128)}, f32[1024,1,3,64]{0,3,2,1:T(8,128)}, f32[16384,64]{0,1:T(8,128)}, f32[16384,64]{0,1:T(8,128)}, s32[]{:T(128)}, /*index=5*/bf16[16384...) while((s32[]{:T(128)}, f32[1024,1,3,64]{0,3,2,1:T(8,128)}, ...), condition=%wide.region_10.11_spmd.clone, body=%wide.region_7.10_spmd.clone.sunk | while | flops 2046232576 | bytes 63893872 | solution.py:44
  118.9 21.2 %conditional.7 = ((f32[1024,1,3,64]{0,3,2,1:T(8,128)}, f32[16384,64]{0,1:T(8,128)}, f32[16384,64]{0,1:T(8,128)})) conditional(s32[]{:T(128)} %convert_element_type.98, (f32[1024,1,3,64]{0,3,2,1:T(8,128)}, f32[16384,64]{0,1:T(8,128)}, f32[16384,64]{0,1:T(8,128)}) %tuple.124, (s32[]{:T(128)}, bf16[16384,64]{0,1:T(8,128)(2,1)}, s32[]{:T(128)}, ...), branch_computations={%region_8.8_spmd, %region_9.9_spmd} | conditional | flops 2046232576 | bytes 63889500 | solution.py:37
  118.9 1.7 broadcast_compare_fusion.1
  120.6 2.7 fusion.36
  123.3 5.9 fusion.19
  129.2 4.9 fusion.30
  134.1 3.3 fusion.24
  137.4 2.7 fusion.26
  140.9 7.5 %pad_maximum_fusion = f32[16384,128]{0,1:T(8,128)} fusion(f32[16384,64]{0,1:T(8,128)} %get-tuple-element.679, f32[16384,64]{0,1:T(8,128)} %get-tuple-element.678), kind=kLoop, calls=%fused_computation.56 | loop fusion | flops 2097152 | bytes 16777216 | tf_op jit(solution)/shard_map/concatenate | solution.py:17
  148.4 1.2 convert_element_type.77
  149.7 0.8 copy.85
  150.5 8.4 %all-to-all-start.6 = ((bf16[8,128,192]{1,2,0:T(8,128)(2,1)}), bf16[8,128,192]{1,2,0:T(8,128)(2,1)S(1)}, u32[]{:S(2)}, u32[]{:S(2)}) async-start(bf16[8,128,192]{1,2,0:T(8,128)(2,1)} %copy.85), calls=%async_computation.6 | async-start | bytes 786432 | tf_op jit(solution)/shard_map/all_to_all | solution.py:175
  159.0 515.2 %reduce-scatter.2.cloned.1.call-done = f32[1024,128]{0,1:T(8,128)} async-done(((f32[16384,128]{0,1:T(8,128)}), f32[1024,128]{0,1:T(8,128)}) %reduce-scatter.2.cloned.1.call-update) | async-done | bytes 524304 | tf_op jit(solution)/shard_map/reduce_scatter | solution.py:19
  674.1 1.1 convert.7
  675.9 6.5 all-to-all-start.8
  683.1 4.6 all-to-all-done.8
  687.6 4.1 all-to-all-start.7
  691.8 0.9 copy.88
  693.5 3.6 all-to-all-done.7
  697.0 0.8 copy.89
  (94 shorter events, 5.4 us)
Async XLA Ops:
  7.2 97.0 %all-gather.2.cloned.1.call-start = ((), (), s32[]{:S(2)}) async-start(), calls=%async_computation.10 | async-start | bytes 2228224 | tf_op jit(solution)/shard_map/all_gather | solution.py:117
  21.7 9.4 %all-to-all-start.2 = ((bf16[128,8,64]{0,2,1:T(8,128)(2,1)}), bf16[128,8,64]{0,2,1:T(8,128)(2,1)S(1)}, u32[]{:S(2)}, u32[]{:S(2)}) async-start(bf16[128,8,64]{0,2,1:T(8,128)(2,1)} %bitcast.30), calls=%async_computation.2 | async-start | bytes 262144 | tf_op jit(solution)/shard_map/all_to_all | solution.py:67
  31.1 12.0 %all-to-all-start.1 = ((bf16[128,8,192]{0,2,1:T(8,128)(2,1)}), bf16[128,8,192]{0,2,1:T(8,128)(2,1)S(1)}, u32[]{:S(2)}, u32[]{:S(2)}) async-start(bf16[128,8,192]{0,2,1:T(8,128)(2,1)} %bitcast.27), calls=%async_computation.1 | async-start | bytes 786432 | tf_op jit(solution)/shard_map/all_to_all | solution.py:55
  43.1 12.3 %all-to-all-start.5 = ((bf16[128,8,192]{0,2,1:T(8,128)(2,1)}), bf16[128,8,192]{0,2,1:T(8,128)(2,1)S(1)}, u32[]{:S(2)}, u32[]{:S(2)}) async-start(bf16[128,8,192]{0,2,1:T(8,128)(2,1)} %bitcast.36), calls=%async_computation.5 | async-start | bytes 786432 | tf_op jit(solution)/shard_map/all_to_all | solution.py:61
  55.4 12.2 %all-to-all-start.4 = ((bf16[128,8,192]{0,2,1:T(8,128)(2,1)}), bf16[128,8,192]{0,2,1:T(8,128)(2,1)S(1)}, u32[]{:S(2)}, u32[]{:S(2)}) async-start(bf16[128,8,192]{0,2,1:T(8,128)(2,1)} %bitcast.33), calls=%async_computation.4 | async-start | bytes 786432 | tf_op jit(solution)/shard_map/all_to_all | solution.py:58
  67.6 1.6 copy-start.1
  69.2 33.4 %all-to-all-start.3 = ((bf16[16,1024,64]{1,2,0:T(8,128)(2,1)}), bf16[16,1024,64]{1,2,0:T(8,128)(2,1)S(1)}, u32[]{:S(2)}, u32[]{:S(2)}) async-start(bf16[16,1024,64]{1,2,0:T(8,128)(2,1)} %stack.3), calls=%async_computation.3 | async-start | bytes 4194304 | tf_op jit(solution)/shard_map/all_to_all | solution.py:119
  76.8 597.3 %reduce-scatter.2.cloned.1.call-start = ((), (), s32[]{:S(2)}) async-start(), calls=%async_computation.11 | async-start | bytes 8912896 | tf_op jit(solution)/shard_map/reduce_scatter | solution.py:19
  104.9 3.6 copy-start
  150.5 525.4 %all-to-all-start.6 = ((bf16[8,128,192]{1,2,0:T(8,128)(2,1)}), bf16[8,128,192]{1,2,0:T(8,128)(2,1)S(1)}, u32[]{:S(2)}, u32[]{:S(2)}) async-start(bf16[8,128,192]{1,2,0:T(8,128)(2,1)} %copy.85), calls=%async_computation.6 | async-start | bytes 786432 | tf_op jit(solution)/shard_map/all_to_all | solution.py:175
  675.9 11.7 %all-to-all-start.8 = ((bf16[8,128,64]{1,2,0:T(8,128)(2,1)}), bf16[8,128,64]{1,2,0:T(8,128)(2,1)S(1)}, u32[]{:S(2)}, u32[]{:S(2)}) async-start(bf16[8,128,64]{1,2,0:T(8,128)(2,1)} %bitcast.185), calls=%async_computation.9 | async-start | bytes 262144 | tf_op jit(solution)/shard_map/all_to_all | solution.py:177
  687.6 9.4 %all-to-all-start.7 = ((bf16[8,128,64]{1,2,0:T(8,128)(2,1)}), bf16[8,128,64]{1,2,0:T(8,128)(2,1)S(1)}, u32[]{:S(2)}, u32[]{:S(2)}) async-start(bf16[8,128,64]{1,2,0:T(8,128)(2,1)} %bitcast.186), calls=%async_computation.8 | async-start | bytes 262144 | tf_op jit(solution)/shard_map/all_to_all | solution.py:176
Sparse Core Ops, SparseCore 0:
  20.2 44.0 all-gather.1
  148.6 525.5 reduce-scatter.1
